TPU v7x, 32 devices: a whole 2x2x4 slice. The times are simulated.
32 devices in a mesh: groups: 2 (over y), seq: 4 (over z), tensor: 2 (over x), cfg: 2 (over core).
Axes of the slice: x: 2, y: 2, z: 4, core: 2. Of those that a mesh axis runs over, the one named last changes fastest.
Arguments:
- latent: bfloat16 [2048, 3072], P(('groups', 'seq')), parts along dimension 0, may hold values from -6 to 6
- positions: int32 [3, 2048], P(None, ('groups', 'seq')), parts along dimension 1, may hold values from 0 to 79, as said below
- text_kv: bfloat16 [2, 2, 128, 3072], P('cfg', None, ('groups', 'seq'), 'tensor'), parts along dimension 2, may hold values from -6 to 6
- text_len: int32 [4], P(('groups', 'cfg')), parts along dimension 0, may hold values from 1 to 64
- modulation: float32 [3, 4, 3072], P(None, 'groups'), parts along dimension 1, may hold values from -3 to 3
- w_qkv: bfloat16 [3, 3072, 3072], P(None, 'cfg', 'tensor'), may hold values from -0.109375 to 0.109375
- norm_gains: float32 [2, 128], replicated, may hold values from 0.5 to 2.5
- w_out: bfloat16 [3072, 3072], P('tensor', 'cfg'), may hold values from -0.109375 to 0.109375
- guidance: float32 [2], P('groups'), parts along dimension 0, may hold values from 3 to 8
Outputs:
- guided: bfloat16 [2048, 3072], P(('groups', 'seq', 'tensor'), 'cfg'), parts along dimension 0
There are 2 independent parts, one for each index of `groups`. A program takes and returns all parts, laid end to end along the dimension named above; an argument that names none is the same for every part. Nothing has to cross between parts.
Inputs may be any that keep to these rules, and one draw needn't show every extreme that they name: `positions`: frame indices are below 33, height indices below 45, width indices below 80. `text_len`: text rows at or beyond the count are ignored.
All inputs are finite; a program needn't handle non-finite values.
Results may differ from a plain program's by a relative error of at most 0.018.
Values may be sent and summed in bfloat16 or wider, within the bound.
A program may use at most 128 MiB of HBM per device.

v0:
```python
import jax
import jax.numpy as jnp
from jax import lax
from jax.sharding import PartitionSpec as P

HEAD_DIM = 128


def swapped(value, axis, apart):
    mask = 2**apart
    pairs = [(source, source ^ mask) for source in range(lax.axis_size(axis))]
    return lax.ppermute(value, axis, pairs)


def head_norm(heads_in, gain):
    return (
        heads_in * lax.rsqrt(jnp.mean(heads_in * heads_in, axis=-1, keepdims=True) + 1e-06) * gain
    )


def rotary(heads_in, positions):
    head_size = heads_in.shape[-1]
    blocks = (head_size // 8, 7 * head_size // 16, 7 * head_size // 16)
    pieces = []
    offset = 0
    for axis_id in range(3):
        width = blocks[axis_id]
        half = width // 2
        freq = 256.0 ** (-jnp.arange(half, dtype=jnp.float32) / half)
        angle = positions[axis_id].astype(jnp.float32)[:, None] * freq[None, :]
        cosine = jnp.cos(angle)[:, None, :]
        sine = jnp.sin(angle)[:, None, :]
        first = heads_in[..., offset : offset + half]
        second = heads_in[..., offset + half : offset + width]
        pieces.append(first * cosine - second * sine)
        pieces.append(second * cosine + first * sine)
        offset = offset + width
    return jnp.concatenate(pieces, axis=-1)


def local(latent, positions, text_kv, text_len, modulation, w_qkv, norm_gains, w_out, guidance):
    rows_here = latent.shape[0]
    width_dev = w_qkv.shape[2]
    heads_dev = width_dev // HEAD_DIM
    text_dev = text_kv.shape[2]
    branch = lax.axis_index("cfg")
    xfloat = latent.astype(jnp.float32)
    center = xfloat - jnp.mean(xfloat, axis=-1, keepdims=True)
    normed = center * lax.rsqrt(jnp.mean(center * center, axis=-1, keepdims=True) + 1e-06)
    both_mod = (
        normed[None] * (1.0 + modulation[1][:, None, :]) + modulation[0][:, None, :]
    ).astype(jnp.bfloat16)
    rows_w = w_qkv.shape[1]
    columns = lax.dynamic_slice_in_dim(both_mod, branch * rows_w, rows_w, 2)
    terms = jnp.einsum("btd,jde->bjte", columns, w_qkv, preferred_element_type=jnp.float32)
    projected = lax.psum_scatter(
        terms.astype(jnp.bfloat16), "cfg", scatter_dimension=0, tiled=True
    ).astype(jnp.float32)[0]
    queries = rotary(
        head_norm(projected[0].reshape(rows_here, heads_dev, HEAD_DIM), norm_gains[0]), positions
    ).astype(jnp.bfloat16)
    keys = rotary(
        head_norm(projected[1].reshape(rows_here, heads_dev, HEAD_DIM), norm_gains[1]), positions
    ).astype(jnp.bfloat16)
    keys = keys.reshape(rows_here, width_dev)
    value_rows = projected[2].astype(jnp.bfloat16)
    text_raw = text_kv[0, 0].astype(jnp.float32).reshape(text_dev, heads_dev, HEAD_DIM)
    text_keys = head_norm(text_raw, norm_gains[1]).astype(jnp.bfloat16).reshape(text_dev, width_dev)
    text_values = text_kv[0, 1]
    length = text_len[0]
    scale = HEAD_DIM ** (-0.5)

    def attend(carry, key_rows, val_rows, valid):
        running_sum, accum = carry
        count = key_rows.shape[0]
        key_heads = key_rows.reshape(count, heads_dev, HEAD_DIM)
        val_heads = val_rows.reshape(count, heads_dev, HEAD_DIM)
        scores = (
            jnp.einsum("thd,nhd->htn", queries, key_heads, preferred_element_type=jnp.float32)
            * scale
        )
        expo = jnp.where(valid[None, None, :], jnp.exp(scores), 0.0)
        new_sum = running_sum + jnp.sum(expo, axis=-1)
        new_acc = accum + jnp.einsum(
            "htn,nhd->htd", expo.astype(jnp.bfloat16), val_heads, preferred_element_type=jnp.float32
        )
        return (new_sum, new_acc)

    start_state = (
        jnp.zeros((heads_dev, rows_here), jnp.float32),
        jnp.zeros((heads_dev, rows_here, HEAD_DIM), jnp.float32),
    )
    carry = start_state
    image_keys = lax.all_gather(keys, "seq", axis=0, tiled=True)
    image_values = lax.all_gather(value_rows, "seq", axis=0, tiled=True)
    prompt_keys = lax.all_gather(text_keys, "seq", axis=0, tiled=True)
    prompt_values = lax.all_gather(text_values, "seq", axis=0, tiled=True)
    carry = attend(carry, image_keys, image_values, jnp.ones((image_keys.shape[0],), bool))
    text_index = jnp.arange(prompt_keys.shape[0], dtype=jnp.int32)
    state = attend(carry, prompt_keys, prompt_values, text_index < length)
    final_sum, final_acc = state
    attended = (
        (final_acc / final_sum[..., None])
        .transpose(1, 0, 2)
        .reshape(rows_here, width_dev)
        .astype(jnp.bfloat16)
    )
    strength = guidance[0]
    half_cols = w_out.shape[1]
    full_out = lax.all_gather(w_out, "cfg", axis=1, tiled=True)
    summed = lax.psum_scatter(
        jnp.dot(attended, full_out, preferred_element_type=jnp.float32).astype(jnp.bfloat16),
        "tensor",
        scatter_dimension=0,
        tiled=True,
    ).astype(jnp.float32)
    gate = lax.dynamic_index_in_dim(modulation[2], branch, 0, keepdims=False)
    mine = (gate * summed).astype(jnp.bfloat16)
    own_half = lax.dynamic_slice_in_dim(mine, branch * half_cols, half_cols, 1)
    send_half = lax.dynamic_slice_in_dim(mine, (1 - branch) * half_cols, half_cols, 1)
    other = swapped(send_half, "cfg", 0)
    cond_rows = jnp.where(branch == 0, own_half, other).astype(jnp.float32)
    uncond_rows = jnp.where(branch == 0, other, own_half).astype(jnp.float32)
    guided = (uncond_rows + strength * (cond_rows - uncond_rows)).astype(jnp.bfloat16)
    return guided


def solution(mesh):
    placed = (
        P(("groups", "seq"), None),
        P(None, ("groups", "seq")),
        P("cfg", None, ("groups", "seq"), "tensor"),
        P(("groups", "cfg")),
        P(None, "groups", None),
        P(None, "cfg", "tensor"),
        P(),
        P("tensor", "cfg"),
        P("groups"),
    )
    return jax.shard_map(
        local,
        mesh=mesh,
        in_specs=placed,
        out_specs=P(("groups", "seq", "tensor"), "cfg"),
        check_vma=False,
    )
```

profile of v0, /device:TPU:0, one launch (start us, length us, event | category | flops | bytes accessed | tf_op | source)
XLA Modules:
  0.0 247.0 jit_solution(18201941797049536414)
XLA Ops:
  6.5 1.5 fusion.31
  8.1 1.7 convert_reduce_fusion
  9.8 0.6 fusion.11
  10.3 2.3 fusion.9
  12.6 1.5 constant_dynamic-slice_fusion.1
  14.1 14.2 %convert_bitcast_fusion = bf16[2,3,256,1536]{3,2,1,0:T(8,128)(2,1)} fusion(bf16[3,1536,1536]{2,1,0:T(8,128)(2,1)} %param.14, f32[2,1536]{1,0:T(2,128)S(1)} %get-tuple-element.46, f32[2,1536]{1,0:T(2,128)S(1)} %get-tuple-element.45, f32[256,1536]{1,0:T(8,128)S(1)} %constant_dynamic-slice_fusion.1), kind=kOutput, calls=%fused_computation.7 | convolution fusion | flops 7252475904 | bytes 20471808 | tf_op jit(solution)/shard_map/btd,jde->bjte/dot_general | solution.py:55
  28.3 0.0 reduce-scatter.3.cloned.1.call-update
  28.3 0.0 copy-start.11
  28.3 0.0 copy-start.12
  28.3 0.0 all-gather.10.cloned.1.call-start
  28.4 15.3 %reduce-scatter.3.cloned.1.call-done = bf16[1,3,256,1536]{3,2,1,0:T(8,128)(2,1)} async-done(((bf16[2,3,256,1536]{3,2,1,0:T(8,128)(2,1)}), bf16[1,3,256,1536]{3,2,1,0:T(8,128)(2,1)}) %reduce-scatter.3.cloned.1.call-update) | async-done | bytes 2359312 | tf_op jit(solution)/shard_map/reduce_scatter | solution.py:56
  43.7 2.3 slice.122
  46.0 0.0 all-gather.10.cloned.1.call-update
  46.0 0.0 all-gather.6.cloned.1.call-start
  46.1 0.1 multiply_cosine_fusion.2
  46.2 0.8 copy.24
  47.0 0.8 copy.25
  47.8 1.5 multiply_cosine_fusion
  49.4 2.0 fusion.30
  51.4 1.9 copy.22
  53.3 1.6 copy.23
  54.9 2.0 copy.26
  56.9 1.6 copy.27
  58.5 0.1 multiply_reduce_fusion.1
  58.7 0.1 multiply_reduce_fusion
  58.8 1.1 copy-done.2
  60.0 0.5 multiply_multiply_fusion.1
  60.4 0.9 copy-done.3
  61.4 0.5 multiply_multiply_fusion
  61.8 0.4 copy-done.5
  62.3 3.3 %add_convert_fusion.1 = (bf16[256,12,28]{2,0,1:T(8,128)(2,1)}, bf16[256,12,28]{2,0,1:T(8,128)(2,1)}, bf16[256,12,28]{2,0,1:T(8,128)(2,1)}, bf16[256,12,28]{2,0,1:T(8,128)(2,1)}) fusion(f32[256,12,128]{2,0,1:T(8,128)S(1)} %multiply_multiply_fusion, f32[256,28]{1,0:T(8,128)S(1)} %get-tuple-element.32, f32[256,28]{1,0:T(8,128)S(1)} %get-tuple-element.31, ...), kind=kLoop, calls=%fused_computation.22 | loop fusion | flops 1376256 | bytes 2179072 | tf_op jit(solution)/shard_map/convert.7
  65.6 2.3 add_convert_fusion.3
  67.9 5.8 %concatenate.9 = bf16[256,12,128]{2,0,1:T(8,128)(2,1)} concatenate(bf16[256,12,8]{2,0,1:T(8,128)(2,1)} %get-tuple-element.12, bf16[256,12,8]{2,0,1:T(8,128)(2,1)} %get-tuple-element.11, bf16[256,12,28]{2,0,1:T(8,128)(2,1)} %get-tuple-element.19, bf16[256,12,28]{2,0,1:T(8,128)(2,1)} %get-tuple-element.20, bf16[256,12,28]{2,0,1:T(8,128)(2,1)} %get-tuple-element.8, ...), dimensions={2} | concatenate | bytes 1572864 | tf_op jit(solution)/shard_map/concatenate | solution.py:38
  73.7 2.3 copy.28
  76.0 0.0 all-gather.6.cloned.1.call-update
  76.0 0.0 all-gather.8.cloned.1.call-start
  76.1 0.5 all-gather.8.cloned.1.call-update
  76.6 0.0 reduce-scatter.5.cloned.1.call-start
  76.7 1.4 slice.107
  78.1 1.4 convert_multiply_fusion
  79.5 1.6 mul.442
  81.8 17.6 %all-gather.1 = bf16[1,1,64,1536]{3,2,1,0:T(8,128)(2,1)} all-gather(bf16[1,1,16,1536]{3,2,1,0:T(8,128)(2,1)} %slice.107), channel_id=3, replica_groups=mesh['groups'=2,'seq'=4,'tensor'=2,'cfg'=2] {'seq'}, dimensions={2}, use_global_device_ids=true | all-gather | bytes 245760 | tf_op jit(solution)/shard_map/all_gather | solution.py:97
  99.4 1.8 reshape.268
  101.2 1.0 reduce_sum.67
  102.2 0.1 mul.443
  102.3 0.8 fusion.28
  103.1 15.8 %all_gather.17 = bf16[64,1536]{1,0:T(8,128)(2,1)} all-gather(bf16[16,1536]{1,0:T(8,128)(2,1)S(1)} %fusion.28), channel_id=1, replica_groups=mesh['groups'=2,'seq'=4,'tensor'=2,'cfg'=2] {'seq'}, dimensions={0}, use_global_device_ids=true | all-gather | bytes 245760 | tf_op jit(solution)/shard_map/all_gather | solution.py:96
  118.9 4.2 %add_convert_fusion.4 = (bf16[256,12,28]{2,0,1:T(8,128)(2,1)}, bf16[256,12,28]{2,0,1:T(8,128)(2,1)}, bf16[256,12,28]{2,0,1:T(8,128)(2,1)}, bf16[256,12,28]{2,0,1:T(8,128)(2,1)}) fusion(f32[256,12,128]{2,0,1:T(8,128)S(1)} %multiply_multiply_fusion.1, f32[256,28]{1,0:T(8,128)S(1)} %get-tuple-element.32, f32[256,28]{1,0:T(8,128)S(1)} %get-tuple-element.31, ...), kind=kLoop, calls=%fused_computation.30 | loop fusion | flops 1376256 | bytes 2179072 | tf_op jit(solution)/shard_map/convert.13
  123.2 4.6 %concatenate.8 = bf16[256,12,128]{2,0,1:T(8,128)(2,1)S(1)} concatenate(bf16[256,12,8]{2,0,1:T(8,128)(2,1)S(1)} %get-tuple-element.23, bf16[256,12,8]{2,0,1:T(8,128)(2,1)S(1)} %get-tuple-element.24, bf16[256,12,28]{2,0,1:T(8,128)(2,1)} %get-tuple-element.21, bf16[256,12,28]{2,0,1:T(8,128)(2,1)} %get-tuple-element.22, bf16[256,12,28]{2,0,1:T(8,128)(2,1)} %get-tuple-element.14, ...), dimensions={2} | concatenate | bytes 1572864 | tf_op jit(solution)/shard_map/concatenate | solution.py:38
  127.8 1.2 fusion.32
  129.0 4.7 %copy.30 = bf16[1,1,1024,1536]{2,3,1,0:T(8,128)(2,1)} copy(bf16[1,1,1024,1536]{3,2,1,0:T(8,128)(2,1)} %all-gather.10.cloned.1.call-done) | data formatting | bytes 6291456 | tf_op jit(solution)/shard_map/all_gather | solution.py:95
  133.7 46.5 %all-gather.6.cloned.1.call-done = bf16[1024,1536]{0,1:T(8,128)(2,1)} async-done(((bf16[256,1536]{0,1:T(8,128)(2,1)}), bf16[1024,1536]{0,1:T(8,128)(2,1)}) %all-gather.6.cloned.1.call-update) | async-done | bytes 3145744 | tf_op jit(solution)/shard_map/all_gather | solution.py:94
  180.2 4.1 %fusion.2 = (f32[12,256]{1,0:T(8,128)S(1)}, f32[12,256,1024]{2,1,0:T(8,128)S(1)}) fusion(bf16[256,12,128]{2,0,1:T(8,128)(2,1)} %copy-done.4, bf16[1024,12,128]{0,2,1:T(8,128)(2,1)} %bitcast.78), kind=kOutput, calls=%fused_computation.3 | convolution fusion | flops 811594752 | bytes 16527360 | tf_op jit(solution)/shard_map/thd,nhd->htn/dot_general | solution.py:79
  184.4 5.6 %fusion.4 = f32[12,256,128]{1,2,0:T(8,128)} fusion(bf16[1024,12,128]{0,2,1:T(8,128)(2,1)} %bitcast.77, f32[12,256,1024]{2,1,0:T(8,128)S(1)} %get-tuple-element.42), kind=kOutput, calls=%fused_computation.5 | convolution fusion | flops 811597824 | bytes 17301504 | tf_op jit(solution)/shard_map/htn,nhd->htd/dot_general | solution.py:84
  190.0 2.4 fusion.17
  192.4 9.1 %all-gather.8.cloned.1.call-done = bf16[1536,3072]{1,0:T(8,128)(2,1)} async-done(((bf16[1536,1536]{1,0:T(8,128)(2,1)}), bf16[1536,3072]{1,0:T(8,128)(2,1)}) %all-gather.8.cloned.1.call-update) | async-done | bytes 9437200 | tf_op jit(solution)/shard_map/all_gather | solution.py:110
  201.5 7.4 %convolution_convert_fusion = bf16[256,3072]{1,0:T(8,128)(2,1)} fusion(bf16[256,1536]{0,1:T(8,128)(2,1)S(1)} %bitcast.80, bf16[1536,3072]{1,0:T(8,128)(2,1)} %all-gather.8.cloned.1.call-done), kind=kOutput, calls=%fused_computation.10 | convolution fusion | flops 2416705536 | bytes 11796480 | tf_op jit(solution)/shard_map/dot_general | solution.py:112
  208.9 0.0 reduce-scatter.5.cloned.1.call-update
  208.9 0.7 copy-done.10
  209.7 26.7 %reduce-scatter.5.cloned.1.call-done = bf16[128,3072]{1,0:T(8,128)(2,1)} async-done(((bf16[256,3072]{1,0:T(8,128)(2,1)}), bf16[128,3072]{1,0:T(8,128)(2,1)}) %reduce-scatter.5.cloned.1.call-update) | async-done | bytes 786448 | tf_op jit(solution)/shard_map/reduce_scatter | solution.py:111
  236.4 1.3 multiply_convert_fusion
  237.7 0.1 collective-permute-start
  238.5 1.1 collective-permute-done
  239.5 0.9 fusion.21
  (37 shorter events, 0.2 us)
Async XLA Ops:
  6.5 3.2 %copy-start = (bf16[256,3072]{1,0:T(8,128)(2,1)S(1)}, bf16[256,3072]{1,0:T(8,128)(2,1)}, u32[]{:S(2)}) copy-start(bf16[256,3072]{1,0:T(8,128)(2,1)} %param.9) | copy-start | bytes 4718596
  6.5 37.2 %reduce-scatter.3.cloned.1.call-start = ((), (), s32[]{:S(2)}) async-start(), calls=%async_computation.2 | async-start | bytes 7077888 | tf_op jit(solution)/shard_map/reduce_scatter | solution.py:56
  28.3 17.8 %copy-start.11 = (s32[3,256]{1,0:T(4,128)S(1)}, s32[3,256]{1,0:T(4,128)}, u32[]{:S(2)}) copy-start(s32[3,256]{1,0:T(4,128)} %param.10) | copy-start | bytes 9220
  28.3 19.5 %copy-start.12 = (f32[2,128]{1,0:T(2,128)S(1)}, f32[2,128]{1,0:T(2,128)}, u32[]{:S(2)}) copy-start(f32[2,128]{1,0:T(2,128)} %param.15) | copy-start | bytes 3076
  28.3 100.7 %all-gather.10.cloned.1.call-start = ((), (), s32[]{:S(2)}) async-start(), calls=%async_computation.6 | async-start | bytes 3932160 | tf_op jit(solution)/shard_map/all_gather | solution.py:95
  43.7 5.7 %copy-start.1 = (bf16[1,3,256,1536]{3,2,1,0:T(8,128)(2,1)S(1)}, bf16[1,3,256,1536]{3,2,1,0:T(8,128)(2,1)}, u32[]{:S(2)}) copy-start(bf16[1,3,256,1536]{3,2,1,0:T(8,128)(2,1)} %reduce-scatter.3.cloned.1.call-done) | copy-start | bytes 7077892
  46.0 134.2 %all-gather.6.cloned.1.call-start = ((), (), s32[]{:S(2)}) async-start(), calls=%async_computation.3 | async-start | bytes 3932160 | tf_op jit(solution)/shard_map/all_gather | solution.py:94
  58.5 1.4 copy-start.2
  60.0 1.4 copy-start.3
  61.4 0.9 copy-start.5
  62.3 3.3 %copy-start.6 = (f32[256,8]{1,0:T(8,128)S(1)}, f32[256,8]{1,0:T(8,128)}, u32[]{:S(2)}) copy-start(f32[256,8]{1,0:T(8,128)} %copy.24) | copy-start | bytes 24580
  62.3 3.3 %copy-start.7 = (f32[256,8]{1,0:T(8,128)S(1)}, f32[256,8]{1,0:T(8,128)}, u32[]{:S(2)}) copy-start(f32[256,8]{1,0:T(8,128)} %copy.25) | copy-start | bytes 24580
  76.0 125.4 %all-gather.8.cloned.1.call-start = ((), (), s32[]{:S(2)}) async-start(), calls=%async_computation.4 | async-start | bytes 14155776 | tf_op jit(solution)/shard_map/all_gather | solution.py:110
  76.6 159.8 %reduce-scatter.5.cloned.1.call-start = ((), (), s32[]{:S(2)}) async-start(), calls=%async_computation.5 | async-start | bytes 2359296 | tf_op jit(solution)/shard_map/reduce_scatter | solution.py:111
  123.2 4.6 %copy-start.9 = (bf16[64,1536]{1,0:T(8,128)(2,1)S(1)}, bf16[64,1536]{1,0:T(8,128)(2,1)}, u32[]{:S(2)}) copy-start(bf16[64,1536]{1,0:T(8,128)(2,1)} %all_gather.17) | copy-start | bytes 589828
  127.8 5.9 %copy-start.4 = (bf16[256,12,128]{2,0,1:T(8,128)(2,1)}, bf16[256,12,128]{2,0,1:T(8,128)(2,1)S(1)}, u32[]{:S(2)}) copy-start(bf16[256,12,128]{2,0,1:T(8,128)(2,1)S(1)} %concatenate.8) | copy-start | bytes 2359300
  184.4 5.6 %copy-start.8 = (bf16[64,12,128]{2,1,0:T(8,128)(2,1)S(1)}, bf16[64,12,128]{2,1,0:T(8,128)(2,1)}, u32[]{:S(2)}) copy-start(bf16[64,12,128]{2,1,0:T(8,128)(2,1)} %reshape.268) | copy-start | bytes 589828
  208.9 0.7 copy-start.10
  237.7 1.8 collective-permute-start
Sparse Core Ops, SparseCore 0:
  28.4 15.2 reduce-scatter.2
  46.1 70.3 all-gather.9
  118.1 62.0 all-gather.5
  181.6 19.7 all-gather.7
  209.0 27.3 reduce-scatter.4
where the time goes:
time: 248 us; the launch traced here: 247 us
  waiting for transfers between devices  99.3 us (40%)
  local copies, waits for them, and re-layouts  40.1 us (16%)
  matrix products  34.9 us (14%)
  blocking collectives  33.4 us (13%)
  other arithmetic  24.3 us (10%)
  between operations  14.7 us (6%)
    all_gather x1, waiting for transfers between devices, local(): image_keys = lax.all_gather(keys, 'seq', axis=0, tiled=True)  46.5 us
    reduce_scatter x1, waiting for transfers between devices, local(): lax.psum_scatter(jnp.dot(attended, full_out, preferred_element_type=jnp.f...  26.7 us
    all_gather x1, blocking collectives, local(): prompt_values = lax.all_gather(text_values, 'seq', axis=0, tiled=True)  17.6 us
    all_gather x1, blocking collectives, local(): prompt_keys = lax.all_gather(text_keys, 'seq', axis=0, tiled=True)  15.8 us
    reduce_scatter x1, waiting for transfers between devices, local(): lax.psum_scatter(terms.astype(jnp.bfloat16), 'cfg', scatter_dimension=0,...  15.3 us
    dot_general x1, matrix products, local(): jnp.einsum('btd,jde->bjte', columns, w_qkv, preferred_element_type=jnp.fl...  14.2 us
    concatenate x3, local copies, waits for them, and re-layouts, rotary(): return jnp.concatenate(pieces, axis=-1)  12.8 us
    another operation x3, other arithmetic  9.86 us
  transfers between devices with their start and end apart: 6, of which 5 were waited for; matrix products, arithmetic and copies ran while one was open for 25% of the time, Pallas kernels for 0%

commit v1 on v0

v1 whole, which is shorter than its diff:
```python
import functools

import jax
import jax.numpy as jnp
import numpy as np
from jax import lax
from jax.experimental import pallas as pl
from jax.experimental.pallas import tpu as pltpu
from jax.sharding import PartitionSpec as P

HEAD_DIM = 128
MESH = pl.DeviceIdType.MESH
F32 = jnp.float32
BF16 = jnp.bfloat16


def rotary_rows(head_size):
    rows = np.zeros((8, head_size), np.float32)
    axes = np.zeros((head_size,), np.int32)
    blocks = (head_size // 8, 7 * head_size // 16, 7 * head_size // 16)
    halves = []
    offset = 0
    for axis_id, width in enumerate(blocks):
        half = width // 2
        if half not in halves:
            halves.append(half)
        which = halves.index(half)
        freq = (256.0 ** (-np.arange(half, dtype=np.float64) / half)).astype(np.float32)
        rows[0, offset : offset + half] = freq
        rows[0, offset + half : offset + width] = freq
        rows[1 + 2 * which, offset : offset + half] = -1.0
        rows[2 + 2 * which, offset + half : offset + width] = 1.0
        axes[offset : offset + width] = axis_id
        offset += width
    shifts = []
    for half in halves:
        shifts += [head_size - half, half]
    return rows, axes, tuple(shifts)


ROT_ROWS, ROT_AXES, ROT_SHIFTS = rotary_rows(HEAD_DIM)


def kernel(
    seq_n,
    ten_n,
    latent,
    pos_lanes,
    text_kv,
    lens_in,
    modulation,
    w_qkv,
    gains,
    w_out,
    mix,
    rot,
    out,
    lat,
    pos,
    txt,
    lens,
    wfull,
    wout,
    mod,
    tab,
    qbuf,
    kbuf,
    vbuf,
    acc,
    lsum,
    attf,
    part,
    got,
    send_a,
    recv_a,
    send_b,
    recv_b,
    send_c,
    recv_c,
    send_p,
    recv_p,
    send_t,
    recv_t,
    send_w,
    recv_w,
    send_l,
    recv_l,
    send_o,
    recv_o,
    send_r,
    recv_r,
    loc,
):
    x = lax.axis_index("tensor")
    c = lax.axis_index("cfg")
    z = lax.axis_index("seq")
    other = 1 - c
    rows, width = latent.shape
    half = w_qkv.shape[1]
    mine = wfull.shape[2]
    heads = mine // HEAD_DIM
    half_rows = rows // 2
    piece = half_rows // ten_n
    out_rows = rows // ten_n
    out_cols = w_out.shape[1]
    scale = HEAD_DIM ** (-0.5)
    tile = 256 if mine % 256 == 0 else 128
    per_tile = tile // HEAD_DIM
    shorter = jnp.minimum(z, seq_n - 1 - z)
    long_sign = jnp.where(2 * z < seq_n - 1, 1, -1)

    def order(i):
        near = i <= 2 * shorter
        dist = jnp.where(near, (i + 1) // 2, i - shorter)
        sign = jnp.where(near, 2 * (i % 2) - 1, long_sign)
        return jnp.where(i == 0, z, z + dist * sign)

    def remote(src, dst, send, recv, **to):
        return pltpu.make_async_remote_copy(
            src_ref=src, dst_ref=dst, send_sem=send, recv_sem=recv, device_id=to, device_id_type=MESH
        )

    def aligned(value, unit):
        return pl.multiple_of(value * unit, unit)

    cols_of = lambda core: pl.ds(aligned(core, mine), mine)
    w_copy = [
        remote(
            w_qkv.at[j, :, cols_of(other)],
            wfull.at[j, pl.ds(aligned(c, half), half), :],
            send_w.at[j],
            recv_w.at[j],
            cfg=other,
        )
        for j in range(3)
    ]
    w_local = [
        pltpu.make_async_copy(
            w_qkv.at[j, :, cols_of(c)], wfull.at[j, pl.ds(aligned(c, half), half), :], loc.at[j]
        )
        for j in range(3)
    ]
    lat_local = pltpu.make_async_copy(latent, lat.at[z], loc.at[3])
    pos_local = pltpu.make_async_copy(pos_lanes, pos.at[z], loc.at[4])
    txt_local = pltpu.make_async_copy(text_kv.at[0, :, :, cols_of(c)], txt.at[c, z], loc.at[5])
    len_local = pltpu.make_async_copy(lens_in, lens.at[c], loc.at[6])
    out_local = pltpu.make_async_copy(w_out, wout, loc.at[7])
    my_piece = pl.ds(pl.multiple_of((c * ten_n + x) * piece, piece), piece)

    def copy_a(i):
        return remote(
            latent.at[my_piece], lat.at[z, my_piece], send_a.at[i], recv_a.at[z], seq=order(i)
        )

    def arrived_a(o):
        return remote(
            latent.at[my_piece], lat.at[o, my_piece], send_a.at[0], recv_a.at[o], seq=order(1)
        )

    def copy_b(o, t):
        to = (x + t) % ten_n
        return remote(
            lat.at[o, my_piece], lat.at[o, my_piece], send_b.at[o, t], recv_b.at[o, t], tensor=to
        )

    def arrived_b(o, t):
        source = (x + ten_n - t) % ten_n
        landed = pl.ds(pl.multiple_of((c * ten_n + source) * piece, piece), piece)
        return remote(
            lat.at[o, landed], lat.at[o, landed], send_b.at[o, t], recv_b.at[o, t], tensor=source
        )

    def copy_c(o, core):
        at = pl.ds(aligned(core, half_rows), half_rows)
        return remote(lat.at[o, at], lat.at[o, at], send_c.at[o], recv_c.at[o], cfg=other)

    def copy_p(i):
        return remote(pos_lanes, pos.at[z], send_p.at[i], recv_p.at[z], seq=order(i))

    def arrived_p(o):
        return remote(pos_lanes, pos.at[o], send_p.at[0], recv_p.at[o], seq=order(1))

    def copy_t(i, core):
        return remote(
            text_kv.at[0, :, :, cols_of(core)],
            txt.at[c, z],
            send_t.at[core, i],
            recv_t.at[c, z],
            seq=order(i),
            cfg=core,
        )

    def copy_t_mirror():
        return remote(
            text_kv.at[0, :, :, cols_of(other)],
            txt.at[c, z],
            send_t.at[other, 0],
            recv_t.at[c, z],
            cfg=other,
        )

    def arrived_t(core, o):
        return remote(
            text_kv.at[0, :, :, cols_of(c)], txt.at[core, o], send_t.at[c, 0], recv_t.at[core, o], cfg=other
        )

    def copy_l(core):
        return remote(lens_in, lens.at[core], send_l.at[0], recv_l.at[0], cfg=other)

    for j in range(3):
        w_local[j].start()
    lat_local.start()
    pos_local.start()
    txt_local.start()
    len_local.start()
    out_local.start()

    barrier = pltpu.get_barrier_semaphore()
    pl.semaphore_signal(barrier, inc=1, device_id={"cfg": other}, device_id_type=MESH)
    for t in range(1, ten_n):
        pl.semaphore_signal(
            barrier, inc=1, device_id={"tensor": (x + t) % ten_n}, device_id_type=MESH
        )
    for s in range(1, seq_n):
        for k in range(2):
            pl.semaphore_signal(
                barrier,
                inc=1,
                device_id={"seq": (z + s) % seq_n, "cfg": (c + k) % 2},
                device_id_type=MESH,
            )
    pl.semaphore_wait(barrier, 1 + (ten_n - 1) + 2 * (seq_n - 1))

    for j in range(3):
        w_copy[j].start()

    @pl.loop(1, seq_n)
    def _(i):
        copy_p(i).start()
        copy_a(i).start()

    copy_l(c).start()
    copy_t_mirror().start()

    @pl.loop(1, seq_n)
    def _(i):
        copy_t(i, 0).start()
        copy_t(i, 1).start()

    acc[...] = jnp.zeros_like(acc)
    lsum[...] = jnp.zeros_like(lsum)
    lat_local.wait()
    pos_local.wait()

    def pump_a(i):
        o = order(i)
        arrived_a(o).wait_recv()
        for t in range(1, ten_n):
            copy_b(o, t).start()

    def pump_b(i):
        o = order(i)
        for t in range(1, ten_n):
            arrived_b(o, t).wait_recv()
        copy_c(o, c).start()

    def normed_head(value, gain):
        return (
            value * lax.rsqrt(jnp.mean(value * value, axis=-1, keepdims=True) + 1e-06) * gain
        )

    def turned(value):
        total = value * tab[0]
        for k, shift in enumerate(ROT_SHIFTS):
            total = total + pltpu.roll(value, shift, 1) * tab[1 + k]
        return total

    def project(j, t):
        at = pl.ds(pl.multiple_of(t * tile, tile), tile)
        return jnp.dot(mod[...], wfull[j, :, at], preferred_element_type=F32)

    def head_tiles(j, gain_row, dest):
        @pl.loop(0, mine // tile)
        def _(t):
            y = project(j, t)
            gain = gains[gain_row : gain_row + 1, :]
            for hh in range(per_tile):
                for b in range(2):
                    part_in = y[b * rows : (b + 1) * rows, hh * HEAD_DIM : (hh + 1) * HEAD_DIM]
                    dest[b * heads + t * per_tile + hh] = turned(normed_head(part_in, gain)).astype(
                        BF16
                    )

    def value_tiles():
        @pl.loop(0, mine // tile)
        def _(t):
            y = project(2, t).astype(BF16)
            for hh in range(per_tile):
                for b in range(2):
                    vbuf[b * heads + t * per_tile + hh] = y[
                        b * rows : (b + 1) * rows, hh * HEAD_DIM : (hh + 1) * HEAD_DIM
                    ]

    strip = 16

    @pl.loop(0, seq_n)
    def _(i):
        o = order(i)

        @pl.when(i > 0)
        def _():
            arrived_p(o).wait_recv()
            copy_c(o, other).wait_recv()

        angle = pos[o].astype(F32) * rot[0:1, :]
        sine = jnp.sin(angle)
        tab[0] = jnp.cos(angle)
        for k in range(len(ROT_SHIFTS)):
            tab[1 + k] = sine * rot[1 + k : 2 + k, :]

        @pl.loop(0, rows // strip)
        def _(r):
            at = pl.ds(pl.multiple_of(r * strip, strip), strip)
            value = lat[o, at, :].astype(F32)
            center = value - jnp.mean(value, axis=-1, keepdims=True)
            normed = center * lax.rsqrt(jnp.mean(center * center, axis=-1, keepdims=True) + 1e-06)
            for b in range(2):
                mod[pl.ds(pl.multiple_of(b * rows + r * strip, strip), strip), :] = (
                    normed * (1.0 + modulation[1, b : b + 1, :]) + modulation[0, b : b + 1, :]
                ).astype(BF16)

        @pl.when(i == 0)
        def _():
            w_local[0].wait()
            w_copy[0].wait_recv()
            head_tiles(0, 0, qbuf)
            w_local[1].wait()
            w_copy[1].wait_recv()
            if seq_n > 1:
                pump_a(1)

        head_tiles(1, 1, kbuf)

        @pl.when(i == 0)
        def _():
            w_local[2].wait()
            w_copy[2].wait_recv()

        value_tiles()

        @pl.when(i + 2 < seq_n)
        def _():
            pump_a(i + 2)

        @pl.when(i + 1 < seq_n)
        def _():
            pump_b(i + 1)

        @pl.loop(0, 2 * heads)
        def _(h):
            scores = lax.dot_general(
                qbuf[h], kbuf[h], (((1,), (1,)), ((), ())), preferred_element_type=F32
            )
            expo = jnp.exp(scores * scale)
            folded = expo[:, :HEAD_DIM]
            for k in range(1, rows // HEAD_DIM):
                folded = folded + expo[:, k * HEAD_DIM : (k + 1) * HEAD_DIM]
            lsum[h] += folded
            acc[h] += jnp.dot(expo.astype(BF16), vbuf[h], preferred_element_type=F32)

    txt_local.wait()
    len_local.wait()
    copy_l(other).wait_recv()
    arrived_t(other, z).wait_recv()

    @pl.loop(1, seq_n)
    def _(i):
        arrived_t(0, order(i)).wait_recv()
        arrived_t(1, order(i)).wait_recv()

    text_rows = txt.shape[3]
    count = seq_n * text_rows
    for b in range(2):
        valid = lax.broadcasted_iota(jnp.int32, (1, count), 1).astype(F32) < lens[b, 0:1, :]

        @pl.loop(0, heads)
        def _(h):
            at = pl.ds(pl.multiple_of(h * HEAD_DIM, HEAD_DIM), HEAD_DIM)
            raw = txt[b, :, 0, :, at].reshape(count, HEAD_DIM).astype(F32)
            keys = normed_head(raw, gains[1:2, :]).astype(BF16)
            values = txt[b, :, 1, :, at].reshape(count, HEAD_DIM)
            n = b * heads + h
            scores = lax.dot_general(
                qbuf[n], keys, (((1,), (1,)), ((), ())), preferred_element_type=F32
            )
            expo = jnp.where(valid, jnp.exp(scores * scale), 0.0)
            total = jnp.sum(lsum[n], axis=-1, keepdims=True) + jnp.sum(
                expo, axis=-1, keepdims=True
            )
            mixed = acc[n] + jnp.dot(expo.astype(BF16), values, preferred_element_type=F32)
            attf[c, b, :, at] = (mixed / total).astype(BF16)

    def copy_o(core):
        return remote(attf.at[core], attf.at[core], send_o.at[0], recv_o.at[0], cfg=other)

    copy_o(c).start()
    out_local.wait()
    copy_o(other).wait_recv()

    def copy_r(t):
        return remote(part.at[t], got.at[t], send_r.at[t], recv_r.at[t], tensor=(x + t) % ten_n)

    out_tile = 256 if out_cols % 256 == 0 else 128

    def out_block(t, at):
        to = (x + t) % ten_n
        here = pl.ds(pl.multiple_of(to * out_rows, out_rows), out_rows)
        total = None
        for b in range(2):
            y = jnp.dot(attf[0, b, here, :], wout[0:mine, at], preferred_element_type=F32)
            y = y + jnp.dot(
                attf[1, b, here, :], wout[mine : 2 * mine, at], preferred_element_type=F32
            )
            y = y * mix[b : b + 1, at]
            total = y if total is None else total + y
        return total

    for t in range(1, ten_n):

        @pl.loop(0, out_cols // out_tile)
        def _(k):
            at = pl.ds(pl.multiple_of(k * out_tile, out_tile), out_tile)
            part[t, :, at] = out_block(t, at).astype(BF16)

        copy_r(t).start()


    @pl.loop(0, out_cols // out_tile)
    def _(k):
        at = pl.ds(pl.multiple_of(k * out_tile, out_tile), out_tile)
        part[0, :, at] = out_block(0, at).astype(BF16)

    for t in range(1, ten_n):
        copy_r(t).wait_recv()
    total = part[0].astype(F32)
    for t in range(1, ten_n):
        total = total + got[t].astype(F32)
    out[...] = total.astype(BF16)

    for j in range(3):
        w_copy[j].wait_send()
    copy_l(c).wait_send()
    copy_t_mirror().wait_send()
    copy_o(c).wait_send()
    for t in range(1, ten_n):
        copy_r(t).wait_send()

    @pl.loop(1, seq_n)
    def _(i):
        copy_p(i).wait_send()
        copy_a(i).wait_send()
        copy_t(i, 0).wait_send()
        copy_t(i, 1).wait_send()
        o = order(i)
        for t in range(1, ten_n):
            copy_b(o, t).wait_send()
        copy_c(o, c).wait_send()


def local(
    seq_n, ten_n, latent, positions, text_kv, text_len, modulation, w_qkv, norm_gains, w_out, guidance
):
    rows, width = latent.shape
    mine = w_qkv.shape[2] // 2
    heads = mine // HEAD_DIM
    text_dev = text_kv.shape[2]
    out_rows = rows // ten_n
    out_cols = w_out.shape[1]
    core = lax.axis_index("cfg")
    axes = jnp.asarray(ROT_AXES)[None, :]
    place = positions.astype(BF16)[:, :, None]
    pos_lanes = jnp.where(axes == 0, place[0], jnp.where(axes == 1, place[1], place[2]))
    lens = jnp.broadcast_to(text_len.astype(F32)[None, :], (8, seq_n * text_dev))
    gate = lax.dynamic_slice_in_dim(modulation[2], core * out_cols, out_cols, 1)
    strength = guidance[0]
    mix = gate * jnp.stack([strength, 1.0 - strength])[:, None]
    any_space = pl.BlockSpec(memory_space=pl.ANY)
    vmem = pl.BlockSpec(memory_space=pltpu.VMEM)
    dma = pltpu.SemaphoreType.DMA
    return pl.pallas_call(
        functools.partial(kernel, seq_n, ten_n),
        out_shape=jax.ShapeDtypeStruct((out_rows, out_cols), BF16),
        in_specs=[
            any_space,
            any_space,
            any_space,
            any_space,
            vmem,
            any_space,
            vmem,
            any_space,
            vmem,
            vmem,
        ],
        out_specs=vmem,
        scratch_shapes=[
            pltpu.VMEM((seq_n, rows, width), BF16),
            pltpu.VMEM((seq_n, rows, HEAD_DIM), BF16),
            pltpu.VMEM((2, seq_n, 2, text_dev, mine), BF16),
            pltpu.VMEM((2, 8, seq_n * text_dev), F32),
            pltpu.VMEM((3, width, mine), BF16),
            pltpu.VMEM(w_out.shape, BF16),
            pltpu.VMEM((2 * rows, width), BF16),
            pltpu.VMEM((1 + len(ROT_SHIFTS), rows, HEAD_DIM), F32),
            pltpu.VMEM((2 * heads, rows, HEAD_DIM), BF16),
            pltpu.VMEM((2 * heads, rows, HEAD_DIM), BF16),
            pltpu.VMEM((2 * heads, rows, HEAD_DIM), BF16),
            pltpu.VMEM((2 * heads, rows, HEAD_DIM), F32),
            pltpu.VMEM((2 * heads, rows, HEAD_DIM), F32),
            pltpu.VMEM((2, 2, rows, mine), BF16),
            pltpu.VMEM((ten_n, out_rows, out_cols), BF16),
            pltpu.VMEM((ten_n, out_rows, out_cols), BF16),
            dma((seq_n,)),
            dma((seq_n,)),
            dma((seq_n, ten_n)),
            dma((seq_n, ten_n)),
            dma((seq_n,)),
            dma((seq_n,)),
            dma((seq_n,)),
            dma((seq_n,)),
            dma((2, seq_n)),
            dma((2, seq_n)),
            dma((3,)),
            dma((3,)),
            dma((1,)),
            dma((1,)),
            dma((1,)),
            dma((1,)),
            dma((ten_n,)),
            dma((ten_n,)),
            dma((8,)),
        ],
        compiler_params=pltpu.CompilerParams(
            collective_id=0, has_side_effects=True, vmem_limit_bytes=64 * 1024 * 1024 - 65536
        ),
    )(
        latent,
        pos_lanes,
        text_kv,
        lens,
        modulation,
        w_qkv,
        norm_gains,
        w_out,
        mix,
        jnp.asarray(ROT_ROWS),
    )


def solution(mesh):
    placed = (
        P(("groups", "seq"), None),
        P(None, ("groups", "seq")),
        P("cfg", None, ("groups", "seq"), "tensor"),
        P(("groups", "cfg")),
        P(None, "groups", None),
        P(None, "cfg", "tensor"),
        P(),
        P("tensor", "cfg"),
        P("groups"),
    )
    return jax.shard_map(
        functools.partial(local, mesh.shape["seq"], mesh.shape["tensor"]),
        mesh=mesh,
        in_specs=placed,
        out_specs=P(("groups", "seq", "tensor"), "cfg"),
        check_vma=False,
    )
```

time: 248 us -> 139 us (0.56)
  Pallas kernels: 0 us -> 131 us
  waiting for transfers between devices: 99.3 us -> 0 us
  local copies, waits for them, and re-layouts: 40.1 us -> 3.12 us
  matrix products: 34.9 us -> 0 us
  blocking collectives: 33.4 us -> 0 us
  other arithmetic: 24.3 us -> 2.9 us
  between operations: 14.7 us -> 1.31 us
    pallas_call x0 -> x1, Pallas kernels: none -> 131 us  [local(): pl.pallas_call(functools.partial(kernel, seq_n, ten_n), out_shape=jax.Sha...]
    all_gather x3 -> x0, waiting for transfers between devices: 55.6 us -> none  [the longest x1 46.5 us: local(): image_keys = lax.all_gather(keys, 'seq', axis=0, tiled=True)]
    reduce_scatter x2 -> x0, waiting for transfers between devices: 42.1 us -> none  [the longest x1 26.7 us: local(): lax.psum_scatter(jnp.dot(attended, full_out, preferred_element_type=jnp.f...]
    dot_general x6 -> x0, matrix products: 34.9 us -> none  [the longest x1 14.2 us: local(): jnp.einsum('btd,jde->bjte', columns, w_qkv, preferred_element_type=jnp.fl...]
    all_gather x2 -> x0, blocking collectives: 33.4 us -> none  [the longest x1 17.6 us: local(): prompt_values = lax.all_gather(text_values, 'seq', axis=0, tiled=True)]
    concatenate x3 -> x0, local copies, waits for them, and re-layouts: 12.8 us -> none  [rotary(): return jnp.concatenate(pieces, axis=-1)]
    another operation x3 -> x1, other arithmetic: 9.86 us -> 0.08 us  [local(): mix = gate * jnp.stack([strength, 1.0 - strength])[:, None]]
    slice x5 -> x2, local copies, waits for them, and re-layouts: 9.56 us -> 0.76 us  [the longest x1 0.74 us: local(): gate = lax.dynamic_slice_in_dim(modulation[2], core * out_cols, out_cols, 1)]
  transfers between devices with their start and end apart: 6 -> 0, of which waited for: 5 -> 0; matrix products, arithmetic and copies ran while one was open for 25% -> 0% of each run, Pallas kernels for 0% -> 0%
where the time goes in v1:
time: 139 us
  Pallas kernels  131 us (94%)
  local copies, waits for them, and re-layouts  3.12 us (2%)
  other arithmetic  2.9 us (2%)
    pallas_call x1, Pallas kernels, local(): pl.pallas_call(functools.partial(kernel, seq_n, ten_n), out_shape=jax.Sha...  131 us

profile of v1, /device:TPU:0, one launch (start us, length us, event | category | flops | bytes accessed | tf_op | source)
XLA Modules:
  0.0 138.6 jit_solution(752174616626915259)
XLA Ops:
  1.3 0.1 pad_maximum_fusion
  1.4 0.7 convert_element_type.6
  2.1 0.6 broadcast_in_dim.66.lens_in
  2.7 0.7 slice.18
  3.4 0.7 bitcast_multiply_fusion.mix
  4.1 1.5 %select_select_fusion.pos_lanes = bf16[256,128]{1,0:T(8,128)(2,1)} fusion(pred[128]{0:T(512)(128)(4,1)} %constant.27, pred[128]{0:T(512)(128)(4,1)} %constant.26, bf16[256]{0:T(256)(128)(2,1)S(1)} %get-tuple-element.6, bf16[256]{0:T(256)(128)(2,1)S(1)} %get-tuple-element.7, bf16[256]{0:T(256)(128)(2,1)S(1)} %get-tuple-element.5), kind=kLoop, calls=%fused_computation | loop fusion | flops 65536 | bytes 67328 | tf_op jit(solution)/shard_map/jit(_where)/select_n | solution.py:482
  5.6 131.2 %shard_map.109 = bf16[128,1536]{1,0:T(8,128)(2,1)} custom-call(bf16[256,3072]{1,0:T(8,128)(2,1)} %latent.1, bf16[256,128]{1,0:T(8,128)(2,1)} %select_select_fusion.pos_lanes, bf16[1,2,16,1536]{3,2,1,0:T(8,128)(2,1)} %text_kv.1, f32[8,64]{1,0:T(8,128)} %broadcast_in_dim.66.lens_in, f32[3,2,3072]{2,1,0:T(2,128)} %modulation.1, bf16[3,1536,1536]{2,1,0:T(8,128)(2,1)} %w_qkv.1, ...), custom_call_target="tpu_custom_call" | custom-call | tf_op jit(solution)/shard_map/pallas_call | solution.py:490
  136.8 1.8 %copy.15 = bf16[128,1536]{1,0:T(8,128)(2,1)} copy(bf16[128,1536]{1,0:T(8,128)(2,1)} %shard_map.109) | data formatting | bytes 786432
  (1 shorter events, 0.0 us)

commit v2 on v1

--- a/solution.py
+++ b/solution.py
@@ -10,6 +10,10 @@
 
 HEAD_DIM = 128
 MESH = pl.DeviceIdType.MESH
+U_TILE = True
+U_MOD = 8
+U_ATT = 4
+U_TEXT = 2
 F32 = jnp.float32
 BF16 = jnp.bfloat16
 
@@ -39,21 +43,23 @@
 
 
 ROT_ROWS, ROT_AXES, ROT_SHIFTS = rotary_rows(HEAD_DIM)
+ROT_PICK = (np.arange(16)[:, None] == ROT_AXES[None, :]).astype(np.float32)
 
 
 def kernel(
     seq_n,
     ten_n,
     latent,
-    pos_lanes,
+    pos_in,
     text_kv,
     lens_in,
     modulation,
     w_qkv,
     gains,
     w_out,
-    mix,
+    guide,
     rot,
+    pick,
     out,
     lat,
     pos,
@@ -141,7 +147,7 @@
         for j in range(3)
     ]
     lat_local = pltpu.make_async_copy(latent, lat.at[z], loc.at[3])
-    pos_local = pltpu.make_async_copy(pos_lanes, pos.at[z], loc.at[4])
+    pos_local = pltpu.make_async_copy(pos_in, pos.at[z], loc.at[4])
     txt_local = pltpu.make_async_copy(text_kv.at[0, :, :, cols_of(c)], txt.at[c, z], loc.at[5])
     len_local = pltpu.make_async_copy(lens_in, lens.at[c], loc.at[6])
     out_local = pltpu.make_async_copy(w_out, wout, loc.at[7])
@@ -175,10 +181,10 @@
         return remote(lat.at[o, at], lat.at[o, at], send_c.at[o], recv_c.at[o], cfg=other)
 
     def copy_p(i):
-        return remote(pos_lanes, pos.at[z], send_p.at[i], recv_p.at[z], seq=order(i))
+        return remote(pos_in, pos.at[z], send_p.at[i], recv_p.at[z], seq=order(i))
 
     def arrived_p(o):
-        return remote(pos_lanes, pos.at[o], send_p.at[0], recv_p.at[o], seq=order(1))
+        return remote(pos_in, pos.at[o], send_p.at[0], recv_p.at[o], seq=order(1))
 
     def copy_t(i, core):
         return remote(
@@ -277,29 +283,30 @@
 
     def project(j, t):
         at = pl.ds(pl.multiple_of(t * tile, tile), tile)
-        return jnp.dot(mod[...], wfull[j, :, at], preferred_element_type=F32)
+        return [
+            jnp.dot(mod[b * rows : (b + 1) * rows, :], wfull[j, :, at], preferred_element_type=F32)
+            for b in range(2)
+        ]
 
     def head_tiles(j, gain_row, dest):
-        @pl.loop(0, mine // tile)
+        @pl.loop(0, mine // tile, unroll=U_TILE)
         def _(t):
             y = project(j, t)
             gain = gains[gain_row : gain_row + 1, :]
             for hh in range(per_tile):
                 for b in range(2):
-                    part_in = y[b * rows : (b + 1) * rows, hh * HEAD_DIM : (hh + 1) * HEAD_DIM]
+                    part_in = y[b][:, hh * HEAD_DIM : (hh + 1) * HEAD_DIM]
                     dest[b * heads + t * per_tile + hh] = turned(normed_head(part_in, gain)).astype(
                         BF16
                     )
 
     def value_tiles():
-        @pl.loop(0, mine // tile)
+        @pl.loop(0, mine // tile, unroll=U_TILE)
         def _(t):
-            y = project(2, t).astype(BF16)
+            y = [value.astype(BF16) for value in project(2, t)]
             for hh in range(per_tile):
                 for b in range(2):
-                    vbuf[b * heads + t * per_tile + hh] = y[
-                        b * rows : (b + 1) * rows, hh * HEAD_DIM : (hh + 1) * HEAD_DIM
-                    ]
+                    vbuf[b * heads + t * per_tile + hh] = y[b][:, hh * HEAD_DIM : (hh + 1) * HEAD_DIM]
 
     strip = 16
 
@@ -312,13 +319,16 @@
             arrived_p(o).wait_recv()
             copy_c(o, other).wait_recv()
 
-        angle = pos[o].astype(F32) * rot[0:1, :]
+        place = lax.dot_general(
+            pos[o], pick[...], (((0,), (0,)), ((), ())), preferred_element_type=F32
+        )
+        angle = place * rot[0:1, :]
         sine = jnp.sin(angle)
         tab[0] = jnp.cos(angle)
         for k in range(len(ROT_SHIFTS)):
             tab[1 + k] = sine * rot[1 + k : 2 + k, :]
 
-        @pl.loop(0, rows // strip)
+        @pl.loop(0, rows // strip, unroll=U_MOD)
         def _(r):
             at = pl.ds(pl.multiple_of(r * strip, strip), strip)
             value = lat[o, at, :].astype(F32)
@@ -348,15 +358,11 @@
 
         value_tiles()
 
-        @pl.when(i + 2 < seq_n)
-        def _():
-            pump_a(i + 2)
-
         @pl.when(i + 1 < seq_n)
         def _():
             pump_b(i + 1)
 
-        @pl.loop(0, 2 * heads)
+        @pl.loop(0, 2 * heads, unroll=U_ATT)
         def _(h):
             scores = lax.dot_general(
                 qbuf[h], kbuf[h], (((1,), (1,)), ((), ())), preferred_element_type=F32
@@ -368,6 +374,10 @@
             lsum[h] += folded
             acc[h] += jnp.dot(expo.astype(BF16), vbuf[h], preferred_element_type=F32)
 
+        @pl.when(i + 2 < seq_n)
+        def _():
+            pump_a(i + 2)
+
     txt_local.wait()
     len_local.wait()
     copy_l(other).wait_recv()
@@ -383,7 +393,7 @@
     for b in range(2):
         valid = lax.broadcasted_iota(jnp.int32, (1, count), 1).astype(F32) < lens[b, 0:1, :]
 
-        @pl.loop(0, heads)
+        @pl.loop(0, heads, unroll=U_TEXT)
         def _(h):
             at = pl.ds(pl.multiple_of(h * HEAD_DIM, HEAD_DIM), HEAD_DIM)
             raw = txt[b, :, 0, :, at].reshape(count, HEAD_DIM).astype(F32)
@@ -412,16 +422,22 @@
 
     out_tile = 256 if out_cols % 256 == 0 else 128
 
-    def out_block(t, at):
+    def out_block(t, k, at):
         to = (x + t) % ten_n
         here = pl.ds(pl.multiple_of(to * out_rows, out_rows), out_rows)
         total = None
+        strength = guide[0:1, 0:1]
+        at_gate = pl.ds(pl.multiple_of(c * out_cols + k * out_tile, out_tile), out_tile)
+        gates = (
+            strength * modulation[2, 0:1, at_gate],
+            (1.0 - strength) * modulation[2, 1:2, at_gate],
+        )
         for b in range(2):
             y = jnp.dot(attf[0, b, here, :], wout[0:mine, at], preferred_element_type=F32)
             y = y + jnp.dot(
                 attf[1, b, here, :], wout[mine : 2 * mine, at], preferred_element_type=F32
             )
-            y = y * mix[b : b + 1, at]
+            y = y * gates[b]
             total = y if total is None else total + y
         return total
 
@@ -430,7 +446,7 @@
         @pl.loop(0, out_cols // out_tile)
         def _(k):
             at = pl.ds(pl.multiple_of(k * out_tile, out_tile), out_tile)
-            part[t, :, at] = out_block(t, at).astype(BF16)
+            part[t, :, at] = out_block(t, k, at).astype(BF16)
 
         copy_r(t).start()
 
@@ -438,7 +454,7 @@
     @pl.loop(0, out_cols // out_tile)
     def _(k):
         at = pl.ds(pl.multiple_of(k * out_tile, out_tile), out_tile)
-        part[0, :, at] = out_block(0, at).astype(BF16)
+        part[0, :, at] = out_block(0, k, at).astype(BF16)
 
     for t in range(1, ten_n):
         copy_r(t).wait_recv()
@@ -476,14 +492,8 @@
     text_dev = text_kv.shape[2]
     out_rows = rows // ten_n
     out_cols = w_out.shape[1]
-    core = lax.axis_index("cfg")
-    axes = jnp.asarray(ROT_AXES)[None, :]
-    place = positions.astype(BF16)[:, :, None]
-    pos_lanes = jnp.where(axes == 0, place[0], jnp.where(axes == 1, place[1], place[2]))
+    pos_in = jnp.pad(positions.astype(BF16), ((0, 13), (0, 0)))
     lens = jnp.broadcast_to(text_len.astype(F32)[None, :], (8, seq_n * text_dev))
-    gate = lax.dynamic_slice_in_dim(modulation[2], core * out_cols, out_cols, 1)
-    strength = guidance[0]
-    mix = gate * jnp.stack([strength, 1.0 - strength])[:, None]
     any_space = pl.BlockSpec(memory_space=pl.ANY)
     vmem = pl.BlockSpec(memory_space=pltpu.VMEM)
     dma = pltpu.SemaphoreType.DMA
@@ -501,11 +511,12 @@
             any_space,
             vmem,
             vmem,
+            vmem,
         ],
         out_specs=vmem,
         scratch_shapes=[
             pltpu.VMEM((seq_n, rows, width), BF16),
-            pltpu.VMEM((seq_n, rows, HEAD_DIM), BF16),
+            pltpu.VMEM((seq_n, 16, rows), BF16),
             pltpu.VMEM((2, seq_n, 2, text_dev, mine), BF16),
             pltpu.VMEM((2, 8, seq_n * text_dev), F32),
             pltpu.VMEM((3, width, mine), BF16),
@@ -545,15 +556,16 @@
         ),
     )(
         latent,
-        pos_lanes,
+        pos_in,
         text_kv,
         lens,
         modulation,
         w_qkv,
         norm_gains,
         w_out,
-        mix,
+        guidance.reshape(1, 1),
         jnp.asarray(ROT_ROWS),
+        jnp.asarray(ROT_PICK, BF16),
     )
 
 

time: 139 us -> 105 us (0.76)
  Pallas kernels: 131 us -> 99.7 us
  other arithmetic: 2.9 us -> 0.69 us
    pallas_call x1, Pallas kernels: 131 us -> 99.7 us  [local(): pl.pallas_call(functools.partial(kernel, seq_n, ten_n), out_shape=jax.Sha...]
    select_n x1 -> x0, other arithmetic: 1.47 us -> none  [local(): jnp.where(axes == 0, place[0], jnp.where(axes == 1, place[1], place[2]))]
where the time goes in v2:
time: 105 us
  Pallas kernels  99.7 us (95%)
  local copies, waits for them, and re-layouts  2.95 us (3%)
  between operations  1.31 us (1%)
    pallas_call x1, Pallas kernels, local(): pl.pallas_call(functools.partial(kernel, seq_n, ten_n), out_shape=jax.Sha...  99.7 us

profile of v2, /device:TPU:0, one launch (start us, length us, event | category | flops | bytes accessed | tf_op | source)
XLA Modules:
  0.0 104.6 jit_solution(14339253362111551334)
XLA Ops:
  1.3 0.7 convert_element_type.8
  2.0 0.6 broadcast_in_dim.9.lens_in
  2.6 0.6 pad.4.pos_in
  3.2 99.7 %shard_map.109 = bf16[128,1536]{1,0:T(8,128)(2,1)} custom-call(bf16[256,3072]{1,0:T(8,128)(2,1)} %latent.1, bf16[16,256]{1,0:T(8,128)(2,1)} %pad.4.pos_in, bf16[1,2,16,1536]{3,2,1,0:T(8,128)(2,1)} %text_kv.1, f32[8,64]{1,0:T(8,128)} %broadcast_in_dim.9.lens_in, f32[3,2,3072]{2,1,0:T(2,128)} %modulation.1, bf16[3,1536,1536]{2,1,0:T(8,128)(2,1)} %w_qkv.1, ...), custom_call_target="tpu_custom_call" | custom-call | tf_op jit(solution)/shard_map/pallas_call | solution.py:500
  102.9 1.8 %copy.15 = bf16[128,1536]{1,0:T(8,128)(2,1)} copy(bf16[128,1536]{1,0:T(8,128)(2,1)} %shard_map.109) | data formatting | bytes 786432
